TPU v7x, 32 devices: a whole 2x2x4 slice. The times are simulated.
32 devices in a mesh: dp: 2 (over x), tp: 16 (over z, y, core).
Axes of the slice: x: 2, y: 2, z: 4, core: 2. Of those that a mesh axis runs over, the one named last changes fastest.
Arguments:
- hidden: bfloat16 [128, 5, 4096], P('dp'), parts along dimension 0
- norm_gain: float32 [4096], replicated
- w_head: bfloat16 [4096, 128256], P(None, 'tp')
- draft_probs: float32 [128, 4, 128256], P('dp', None, 'tp'), parts along dimension 0
- draft_tokens: int32 [128, 4], P('dp'), parts along dimension 0
- temperature: float32 [128], P('dp'), parts along dimension 0
Outputs:
- output 1: float32 [128, 4], P('dp'), parts along dimension 0
- output 2: float32 [128, 4], P('dp'), parts along dimension 0
- output 3: float32 [128, 4, 128256], P('dp', None, 'tp'), parts along dimension 0
- output 4: float32 [128], P('dp'), parts along dimension 0
There are 2 independent parts. A program takes and returns all parts, laid end to end along the dimension named above; an argument that names none is the same for every part.
All inputs are finite; a program needn't handle non-finite values.
Results may differ from a plain program's by a relative error of at most 0.001.
Values sent between devices are 32-bit elements.
A program may use at most 1 GiB of HBM per device.

v0:
```python
import jax
import jax.numpy as jnp
from jax import lax
from jax.sharding import PartitionSpec as P


def solution(mesh):
    def local_step(hidden, norm_gain, w_head, draft_probs, draft_tokens, value_a11):
        draft_len = draft_probs.shape[1]
        shard_vocab = w_head.shape[1]
        hidden_f32 = hidden.astype(jnp.float32)
        inv_rms = lax.rsqrt(jnp.mean(hidden_f32 * hidden_f32, axis=-1, keepdims=True) + 1e-5)
        normed = (hidden_f32 * inv_rms * norm_gain).astype(jnp.bfloat16)
        logits = jnp.einsum('cle,ew->clw', normed, w_head, preferred_element_type=jnp.float32)
        scaled = logits / value_a11[:, None, None]
        row_max = lax.pmax(jnp.max(scaled, axis=-1), 'tp')
        local_sum = jnp.sum(jnp.exp(scaled - row_max[:, :, None]), axis=-1)
        local_idx = draft_tokens - lax.axis_index('tp') * shard_vocab
        is_owned = (local_idx >= 0) & (local_idx < shard_vocab)
        safe_idx = jnp.clip(local_idx, 0, shard_vocab - 1)[:, :, None]
        tok_scaled = jnp.where(is_owned, jnp.take_along_axis(scaled[:, :draft_len], safe_idx, axis=-1)[:, :, 0], 0.0)
        tok_draft = jnp.where(is_owned, jnp.take_along_axis(draft_probs, safe_idx, axis=-1)[:, :, 0], 0.0)
        total_sum, tok_scaled, tok_draft = lax.psum((local_sum, tok_scaled, tok_draft), 'tp')
        row_lse = row_max + jnp.log(total_sum)
        draft_lse = row_lse[:, :draft_len]
        tok_target = jnp.exp(tok_scaled - draft_lse)
        accept = jnp.minimum(1.0, tok_target / tok_draft)
        excess = jnp.maximum(jnp.exp(scaled[:, :draft_len] - draft_lse[:, :, None]) - draft_probs, 0.0)
        norm_sum = lax.psum(jnp.sum(excess, axis=-1), 'tp')
        residual = excess / norm_sum[:, :, None]
        return accept, norm_sum, residual, row_lse[:, draft_len]

    return jax.shard_map(
        local_step,
        mesh=mesh,
        in_specs=(P('dp', None, None), P(), P(None, 'tp'), P('dp', None, 'tp'), P('dp', None), P('dp')),
        out_specs=(P('dp', None), P('dp', None), P('dp', None, 'tp'), P('dp')),
        check_vma=False,
    )
```

profile of v0, /device:TPU:0, one launch (start us, length us, event | category | flops | bytes accessed | tf_op | source)
XLA Modules:
  0.0 182.0 jit_solution(8430714029817135250)
XLA Ops:
  0.6 0.7 fusion.19
  1.4 2.3 %fusion.6 = f32[64,5]{0,1:T(8,128)S(1)} fusion(bf16[64,5,4096]{2,0,1:T(8,128)(2,1)} %param.8), kind=kLoop, calls=%fused_computation.10 | loop fusion | flops 3931840 | bytes 2622720 | tf_op jit(solution)/shard_map/reduce_sum | solution.py:12
  3.7 0.1 copy.24
  3.8 0.1 reshape.58
  3.9 0.0 copy-start
  3.9 0.0 copy-start.3
  3.9 0.0 copy-start.4
  3.9 4.1 %gather_fusion.1 = f32[256]{0:T(256)S(1)} fusion(f32[64,4,8016]{2,1,0:T(4,128)} %param.11, s32[256]{0:T(256)S(1)} %reshape.58), kind=kCustom, calls=%fused_computation.1.clone | custom fusion | bytes 5120 | tf_op jit(solution)/shard_map/jit(take_along_axis)/gather | solution.py:22
  8.1 0.1 reshape.67
  8.2 0.1 copy.27
  8.2 0.0 copy-done
  8.2 0.0 copy-done.3
  8.2 0.0 copy-done.4
  8.3 34.1 %fusion.20 = (f32[64,5]{0,1:T(8,128)S(1)}, f32[64,5,8016]{2,0,1:T(8,128)}) fusion(f32[64]{0:T(128)S(1)} %copy-done.4, bf16[4096,8016]{0,1:T(8,128)(2,1)} %param.10, bf16[64,5,4096]{2,0,1:T(8,128)(2,1)S(1)} %copy-done, f32[4096]{0:T(1024)S(1)} %copy-done.3, f32[64,5]{0,1:T(8,128)S(1)} %add_rsqrt_fusion), kind=kOutput, calls=%fused_computation.37 | convolution fusion | flops 21023834112 | bytes 78568192 | tf_op jit(solution)/shard_map/cle,ew->clw/dot_general | solution.py:14
  42.4 35.0 %pmax.7 = f32[64,5]{0,1:T(8,128)S(1)} all-reduce(f32[64,5]{0,1:T(8,128)S(1)} %get-tuple-element.29), channel_id=1, replica_groups=mesh['dp'=2,'tp'=16] {'tp'}, use_global_device_ids=true, to_apply=%region_3.5 | all-reduce | flops 320 | bytes 2560 | tf_op jit(solution)/shard_map/pmax | solution.py:16
  77.4 5.4 %exponential_reduce_fusion = f32[64,5]{0,1:T(8,128)S(1)} fusion(f32[64,5,8016]{2,0,1:T(8,128)} %get-tuple-element.30, f32[64,5]{0,1:T(8,128)S(1)} %pmax.7), kind=kLoop, calls=%fused_computation.4 | loop fusion | flops 5129920 | bytes 10263040 | tf_op jit(solution)/shard_map/reduce_sum | solution.py:17
  82.8 29.5 %psum.29 = f32[64,5]{0,1:T(8,128)S(1)} all-reduce(f32[64,5]{0,1:T(8,128)S(1)} %exponential_reduce_fusion), channel_id=1, replica_groups=mesh['dp'=2,'tp'=16] {'tp'}, use_global_device_ids=true, to_apply=%region_5.7 | all-reduce | flops 320 | bytes 2560 | tf_op jit(solution)/shard_map/psum | solution.py:23
  112.3 0.5 slice_bitcast_fusion
  112.8 12.7 %fusion.12 = (f32[64,4]{0,1:T(4,128)S(1)}, f32[64,4,8016]{2,0,1:T(8,128)}) fusion(f32[64,4,8016]{2,1,0:T(4,128)} %param.11, f32[64,4]{0,1:T(4,128)S(1)} %slice.11, f32[64,5,8016]{2,0,1:T(8,128)} %get-tuple-element.30), kind=kLoop, calls=%fused_computation.16 | loop fusion | flops 8208128 | bytes 24627200 | tf_op jit(solution)/shard_map/reduce_sum | solution.py:29
  125.5 0.0 copy-start.1
  125.5 4.3 %gather_fusion = f32[256]{0:T(256)S(1)} fusion(f32[64,4,8016]{2,0,1:T(8,128)} %get-tuple-element.28, s32[256]{0:T(256)S(1)} %reshape.58), kind=kCustom, calls=%fused_computation.clone | custom fusion | bytes 5120 | tf_op jit(solution)/shard_map/jit(take_along_axis)/gather | solution.py:21
  129.8 0.1 reshape.61
  129.9 0.1 copy.25
  129.9 0.0 copy-done.1
  130.0 30.2 %all-reduce = (f32[64,4]{0,1:T(4,128)S(1)}, f32[64,4]{0,1:T(4,128)S(1)}, f32[64,4]{0,1:T(4,128)S(1)}) all-reduce(f32[64,4]{0,1:T(4,128)S(1)} %bitcast_select_fusion, f32[64,4]{0,1:T(4,128)S(1)} %get-tuple-element.24, f32[64,4]{0,1:T(4,128)S(1)} %get-tuple-element.27), channel_id=1, replica_groups=mesh['dp'=2,'tp'=16] {'tp'}, use_global_device_ids=true, to_apply=%region_6.8 | all-reduce | flops 768 | bytes 6144 | tf_op jit(solution)/shard_map/psum | solution.py:23
  160.1 0.0 copy-start.2
  160.2 9.3 %broadcast_divide_fusion = f32[64,4,8016]{2,0,1:T(8,128)} fusion(f32[64,4]{0,1:T(4,128)S(1)} %get-tuple-element.23, f32[64,4,8016]{2,1,0:T(4,128)} %param.11, f32[64,4]{0,1:T(4,128)S(1)} %slice.11, f32[64,5,8016]{2,0,1:T(8,128)} %get-tuple-element.30), kind=kLoop, calls=%fused_computation.13 | loop fusion | flops 8208384 | bytes 24627200 | tf_op jit(solution)/shard_map/div | solution.py:30
  169.4 0.0 copy-done.2
  169.4 12.0 %copy.29 = f32[64,4,8016]{2,1,0:T(4,128)} copy(f32[64,4,8016]{2,0,1:T(8,128)} %broadcast_divide_fusion) | data formatting | bytes 16416768
  181.4 0.6 fusion.18
  (9 shorter events, 0.1 us)
Async XLA Ops:
  3.9 4.3 %copy-start = (bf16[64,5,4096]{2,0,1:T(8,128)(2,1)S(1)}, bf16[64,5,4096]{2,0,1:T(8,128)(2,1)}, u32[]{:S(2)}) copy-start(bf16[64,5,4096]{2,0,1:T(8,128)(2,1)} %param.8) | copy-start | bytes 7864324
  3.9 4.3 %copy-start.3 = (f32[4096]{0:T(1024)S(1)}, f32[4096]{0:T(1024)}, u32[]{:S(2)}) copy-start(f32[4096]{0:T(1024)} %param.9) | copy-start | bytes 49156
  3.9 4.3 %copy-start.4 = (f32[64]{0:T(128)S(1)}, f32[64]{0:T(128)}, u32[]{:S(2)}) copy-start(f32[64]{0:T(128)} %param.13) | copy-start | bytes 772
  125.5 4.5 %copy-start.1 = (s32[64,4]{0,1:T(4,128)S(1)}, s32[64,4]{0,1:T(4,128)}, u32[]{:S(2)}) copy-start(s32[64,4]{0,1:T(4,128)} %param.12) | copy-start | bytes 3076
  160.1 9.3 %copy-start.2 = (f32[64,4]{0,1:T(4,128)}, f32[64,4]{0,1:T(4,128)S(1)}, u32[]{:S(2)}) copy-start(f32[64,4]{0,1:T(4,128)S(1)} %get-tuple-element.23) | copy-start | bytes 3076
where the time goes:
time: 183 us; the launch traced here: 182 us
  blocking collectives  94.6 us (52%)
  matrix products  34.1 us (19%)
  other arithmetic  31 us (17%)
  local copies, waits for them, and re-layouts  21.5 us (12%)
    psum x2, blocking collectives, local_step(): lax.psum((local_sum, tok_scaled, tok_draft), 'tp')  59.6 us
    pmax x1, blocking collectives, local_step(): row_max = lax.pmax(jnp.max(scaled, axis=-1), 'tp')  35 us
    dot_general x1, matrix products, local_step(): jnp.einsum('cle,ew->clw', normed, w_head, preferred_element_type=jnp.floa...  34.1 us
    reduce_sum x1, other arithmetic, local_step(): norm_sum = lax.psum(jnp.sum(excess, axis=-1), 'tp')  12.7 us
    unnamed x11, local copies, waits for them, and re-layouts  12 us
    div x1, other arithmetic, local_step(): residual = excess / norm_sum[:, :, None]  9.26 us
    reduce_sum x1, other arithmetic, local_step(): local_sum = jnp.sum(jnp.exp(scaled - row_max[:, :, None]), axis=-1)  5.44 us
    gather x5, local copies, waits for them, and re-layouts, local_step(): jnp.take_along_axis(scaled[:, :draft_len], safe_idx, axis=-1)[:, :, 0]  4.68 us

commit v1 on v0

v1 whole, which is shorter than its diff:
```python
import functools

import jax
import jax.numpy as jnp
from jax import lax
from jax.experimental import pallas as pl
from jax.experimental.pallas import tpu as pltpu
from jax.sharding import PartitionSpec as P

MESH = pl.DeviceIdType.MESH
F32 = jnp.float32
BF16 = jnp.bfloat16
LOG2E = 1.4426950408889634
LN2 = 0.6931471805599453
NEG = -1e30
LANES = 128
TILE = 256
BLOCK = 2 * TILE
SLOTS = 6
PIECE = 64


def stream_trips(vocab):
    return vocab // (2 * BLOCK)


def column(row):
    return jnp.transpose(jnp.broadcast_to(row, (LANES, LANES)))


def stream_kernel(dims, hid_ref, gain_ref, wt_ref, q_ref, meta_ref,
                  qb, zs, xb, wtail, mx, sm, tk, tokc, invc,
                  hid, xs, ring, hid_sem, w_sem, q_sem, t_sem):
    seqs, draft, depth, vocab = dims
    rows = seqs * draft
    total = rows + seqs
    ktiles = depth // TILE
    trips = stream_trips(vocab)
    nblocks = 2 * trips
    tail = vocab - nblocks * BLOCK
    pieces = total // PIECE

    def w_copy(block):
        slot = lax.rem(block, SLOTS)
        return pltpu.make_async_copy(
            wt_ref.at[pl.ds(pl.multiple_of(block * BLOCK, BLOCK), BLOCK), :], ring.at[slot], w_sem.at[slot])

    tail_copy = pltpu.make_async_copy(wt_ref.at[pl.ds(nblocks * BLOCK, tail), :], wtail, t_sem)

    hid_copy = pltpu.make_async_copy(hid_ref, hid, hid_sem)
    hid_copy.start()
    for i in range(SLOTS):
        w_copy(i).start()

    mx[...] = jnp.full(mx.shape, NEG, F32)
    sm[...] = jnp.ones(sm.shape, F32)
    tk[...] = jnp.zeros(tk.shape, F32)
    invc[pl.ds(0, LANES), :] = column(meta_ref[0:1, :])
    invc[pl.ds(LANES, LANES), :] = column(meta_ref[1:2, :])
    invc[pl.ds(2 * LANES, PIECE), :] = column(meta_ref[2:3, :])[0:PIECE, :]
    tokc[pl.ds(0, LANES), :] = column(meta_ref[3:4, :])
    tokc[pl.ds(LANES, LANES), :] = column(meta_ref[4:5, :])

    hid_copy.wait()
    chunks = depth // LANES

    def squares(c, accs):
        out = []
        for j in range(draft + 1):
            h = hid[j, :, pl.ds(pl.multiple_of(c * LANES, LANES), LANES)].astype(F32)
            out.append(accs[j] + h * h)
        return tuple(out)

    sums = lax.fori_loop(0, chunks, squares, tuple(jnp.zeros((seqs, LANES), F32) for _ in range(draft + 1)))
    invr = [jnp.broadcast_to(lax.rsqrt(jnp.sum(s, axis=-1, keepdims=True) * (1.0 / depth) + 1e-5), (seqs, LANES))
            for s in sums]

    def normalise(c, carry):
        lanes = pl.ds(pl.multiple_of(c * LANES, LANES), LANES)
        g = gain_ref[:, lanes]
        slab = lax.rem(c, 2)
        for j in range(draft + 1):
            x = hid[j, :, lanes].astype(F32) * carry[j] * g
            if j < draft:
                xs[slab, pl.ds(j, seqs, stride=draft), :] = x
            else:
                xs[slab, pl.ds(rows, seqs), :] = x
        xb[:, lanes] = xs[slab].astype(BF16)
        return carry

    lax.fori_loop(0, chunks, normalise, tuple(invr))

    lane = lax.broadcasted_iota(jnp.int32, (8, LANES), 1)

    per = 8

    def stream(*accs):
        acc = [[accs[(par * 2 + q) * pieces:(par * 2 + q + 1) * pieces] for q in range(2)] for par in range(2)]

        def push(slot, k, q):
            pltpu.matmul_push_rhs(ring[slot, q * TILE:(q + 1) * TILE, k * TILE:(k + 1) * TILE],
                                  staging_register=k % 2, mxu_index=q, transpose=True)

        def process(par, block):
            limit = jnp.where(block < 0, 0, BLOCK)
            base = block * BLOCK
            for p in range(pieces):
                z = [pltpu.matmul_pop(acc[par][q][p]) for q in range(2)]
                r = pl.ds(p * PIECE, PIECE)
                inv = invc[r, :]
                s = []
                for g in range(4):
                    v = z[g // 2][:, (g % 2) * LANES:(g % 2 + 1) * LANES] * inv
                    ok = jnp.broadcast_to((lane + g * LANES < limit)[0:1], (PIECE, LANES))
                    v = jnp.where(ok, v, NEG)
                    s.append(v)
                if (p + 1) * PIECE <= rows:
                    t = tk[r, :]
                    tokr = tokc[r, :]
                    for g in range(4):
                        col = (lane + (base + g * LANES)).astype(F32)[0:1]
                        t = t + jnp.where(tokr == col, s[g], 0.0)
                        zs[r, pl.ds(pl.multiple_of((block + 1) * BLOCK + g * LANES, LANES), LANES)] = s[g]
                    tk[r, :] = t
                m_old = mx[r, :]
                m_new = jnp.maximum(jnp.maximum(m_old, jnp.maximum(s[0], s[1])), jnp.maximum(s[2], s[3]))
                e = sm[r, :] * jnp.exp2(m_old - m_new)
                e = e + ((jnp.exp2(s[0] - m_new) + jnp.exp2(s[1] - m_new))
                         + (jnp.exp2(s[2] - m_new) + jnp.exp2(s[3] - m_new)))
                mx[r, :] = m_new
                sm[r, :] = e

        def half(trip, par):
            block = trip * 2 + par
            slot = lax.rem(block, SLOTS)
            after = lax.rem(block + 1, SLOTS)
            for k in range(ktiles):
                if k == ktiles - 2:
                    if par == 0:
                        w_copy(block + 1).wait()
                    else:
                        @pl.when(trip < trips - 1)
                        def _():
                            w_copy(block + 1).wait()
                    fresh = block - 1 + SLOTS

                    @pl.when((block >= 1) & (fresh < nblocks))
                    def _():
                        w_copy(fresh).start()

                    @pl.when(fresh == nblocks)
                    def _():
                        tail_copy.start()

                    @pl.when(block < seqs // per)
                    def _():
                        for i in range(per):
                            pltpu.make_async_copy(
                                q_ref.at[block * per + i],
                                qb.at[pl.ds(pl.multiple_of(block * per * draft, 8) + i * draft, draft), :],
                                q_sem.at[block * per + i]).start()
                for q in range(2):
                    if k + 1 < ktiles:
                        push(slot, k + 1, q)
                    else:
                        push(after, 0, q)
                for p in range(pieces):
                    x = xb[p * PIECE:(p + 1) * PIECE, k * TILE:(k + 1) * TILE]
                    for q in range(2):
                        pltpu.matmul_acc_lhs(acc[par][q][p], x, load_staged_rhs=(k % 2) if p == 0 else None)
                if k == 1:
                    process(1 - par, block - 1)

        for a in accs:
            pltpu.matmul_pop(a)
        w_copy(0).wait()
        for q in range(2):
            push(0, 0, q)

        @pl.loop(0, trips)
        def _(trip):
            half(trip, 0)
            half(trip, 1)

        zero = jnp.zeros((16, TILE), BF16)
        for q in range(2):
            pltpu.matmul_acc_lhs(acc[0][q][0], jnp.zeros((PIECE, TILE), BF16), load_staged_rhs=0)
        process(1, nblocks - 1)
        for q in range(2):
            pltpu.matmul_pop(acc[0][q][0])

    pl.run_scoped(stream, *[pltpu.ACC(q)((PIECE, TILE), F32)
                            for _ in range(2) for q in range(2) for _ in range(pieces)])

    tail_copy.wait()
    for b in range(seqs):
        pltpu.make_async_copy(q_ref.at[b], qb.at[pl.ds(b * draft, draft), :], q_sem.at[b]).wait()


def exchange_kernel(dims, n, q_ref, zs_ref, xb_ref, wtail_ref, mx_ref, sm_ref, tk_ref, tokc_ref, invc_ref, meta_ref,
                    zt, lcol, stat_ref, icol_ref,
                    mx, sm, tk, qcol, send1, recv1, send2, recv2, s1_sem, r1_sem, s2_sem, r2_sem):
    seqs, draft, depth, vocab = dims
    rows = seqs * draft
    total = rows + seqs
    me = lax.axis_index("tp")
    first_tail = 2 * stream_trips(vocab) * BLOCK
    tail = vocab - first_tail
    vtiles = pl.cdiv(vocab, LANES)
    lane = lax.broadcasted_iota(jnp.int32, (8, LANES), 1)

    barrier = pltpu.get_barrier_semaphore()
    for d in range(1, n):
        pl.semaphore_signal(barrier, inc=1, device_id={"tp": lax.rem(me + d, n)}, device_id_type=MESH)

    zt[:, :tail] = lax.dot_general(xb_ref[...], wtail_ref[...], (((1,), (1,)), ((), ())),
                                   preferred_element_type=F32)
    mx[...] = mx_ref[...]
    sm[...] = sm_ref[...]
    tk[...] = tk_ref[...]
    step = 32
    ttiles = pl.cdiv(tail, LANES)

    def finish(i, is_draft):
        r = pl.ds(pl.multiple_of(i * step, step), step)
        inv = invc_ref[r, :]
        s = []
        for g in range(ttiles):
            v = zt[r, g * LANES:(g + 1) * LANES] * inv
            if (g + 1) * LANES > tail:
                v = jnp.where(jnp.broadcast_to((lane + g * LANES < tail)[0:1], (step, LANES)), v, NEG)
            s.append(v)
        if is_draft:
            t = tk[r, :]
            tokr = tokc_ref[r, :]
            for g in range(ttiles):
                col = (lane + (first_tail + g * LANES)).astype(F32)[0:1]
                t = t + jnp.where(tokr == col, s[g], 0.0)
                zt[r, g * LANES:(g + 1) * LANES] = s[g]
            tk[r, :] = t
        m_old = mx[r, :]
        m_new = functools.reduce(jnp.maximum, s, m_old)
        e = sm[r, :] * jnp.exp2(m_old - m_new)
        for v in s:
            e = e + jnp.exp2(v - m_new)
        mx[r, :] = m_new
        sm[r, :] = e

    @pl.loop(0, rows // step)
    def _(i):
        finish(i, True)

    @pl.loop(rows // step, total // step)
    def _(i):
        finish(i, False)

    lse = []
    for blk in range(3):
        r = pl.ds(blk * LANES, LANES)
        mt = jnp.transpose(mx[r, :])
        st = jnp.transpose(sm[r, :])
        top = jnp.max(mt, axis=0, keepdims=True)
        tot = jnp.sum(st * jnp.exp2(mt - top), axis=0, keepdims=True)
        lse.append(top + jnp.log(tot) * LOG2E)
    for blk in range(3):
        send1[blk:blk + 1, :] = lse[blk]
        recv1[me, blk:blk + 1, :] = lse[blk]
    send1[3:4, :] = lse[2]
    recv1[me, 3:4, :] = lse[2]

    pl.semaphore_wait(barrier, n - 1)

    def exchange(send, recv, s_sem, r_sem):
        return [pltpu.make_async_remote_copy(
            src_ref=send, dst_ref=recv.at[me], send_sem=s_sem.at[d], recv_sem=r_sem.at[d],
            device_id={"tp": lax.rem(me + d, n)}, device_id_type=MESH) for d in range(1, n)]

    first = exchange(send1, recv1, s1_sem, r1_sem)
    for c in first:
        c.start()

    group = 32

    def gather(i, carry):
        r = pl.ds(pl.multiple_of(i * group, group), group)
        tokr = tokc_ref[r, :]
        acc = jnp.zeros((group, LANES), F32)
        for v in range(vtiles):
            size = min(LANES, vocab - v * LANES)
            col = (lane + v * LANES).astype(F32)[0:1]
            if size == LANES:
                acc = acc + jnp.where(tokr == col, q_ref[r, v * LANES:(v + 1) * LANES], 0.0)
            else:
                acc_t = jnp.where(tokr[:, :size] == col[:, :size], q_ref[r, v * LANES:v * LANES + size], 0.0)
                acc = acc + jnp.pad(acc_t, ((0, 0), (0, LANES - size)))
        qcol[r, :] = acc
        return carry

    lax.fori_loop(0, rows // group, gather, 0)
    tok_q = [jnp.sum(jnp.transpose(qcol[pl.ds(i * LANES, LANES), :]), axis=0, keepdims=True) for i in range(2)]
    tok_s = [jnp.sum(jnp.transpose(tk[pl.ds(i * LANES, LANES), :]), axis=0, keepdims=True) for i in range(2)]

    for c in first:
        c.wait()

    parts = [recv1[i] for i in range(n)]
    top = functools.reduce(jnp.maximum, parts)
    tot = functools.reduce(jnp.add, [jnp.exp2(x - top) for x in parts])
    full = top + jnp.log(tot) * LOG2E
    for i in range(2):
        lcol[pl.ds(i * LANES, LANES), :] = column(full[i:i + 1, :])

    def excess(i, carry):
        r = pl.ds(pl.multiple_of(i * group, group), group)
        lr = lcol[r, :]
        acc = jnp.zeros((group, LANES), F32)
        for v in range(vtiles):
            size = min(LANES, vocab - v * LANES)
            off = v * LANES - first_tail
            s = zs_ref[r, BLOCK + v * LANES:BLOCK + (v + 1) * LANES] if off < 0 else zt[r, off:off + LANES]
            e = jnp.maximum(jnp.exp2(s - lr)[:, :size] - q_ref[r, v * LANES:v * LANES + size], 0.0)
            acc = acc + (e if size == LANES else jnp.pad(e, ((0, 0), (0, LANES - size))))
        tk[r, :] = acc
        return carry

    lax.fori_loop(0, rows // group, excess, 0)

    for i in range(2):
        part = jnp.sum(jnp.transpose(tk[pl.ds(i * LANES, LANES), :]), axis=0, keepdims=True)
        tok = meta_ref[3 + i:4 + i, :]
        owned = (tok >= 0.0) & (tok < float(vocab))
        ratio = jnp.minimum(1.0, jnp.exp2(tok_s[i] - full[i:i + 1, :]) / jnp.where(owned, tok_q[i], 1.0))
        ratio = jnp.where(owned, ratio, 0.0)
        send2[i:i + 1, :] = part
        send2[2 + i:3 + i, :] = ratio
        recv2[me, i:i + 1, :] = part
        recv2[me, 2 + i:3 + i, :] = ratio

    second = exchange(send2, recv2, s2_sem, r2_sem)
    for c in second:
        c.start()
    for c in second:
        c.wait()
    summed = functools.reduce(jnp.add, [recv2[i] for i in range(n)])
    stat_ref[0:4, :] = summed
    stat_ref[4:8, :] = full * LN2
    for i in range(2):
        icol_ref[pl.ds(i * LANES, LANES), :] = column(1.0 / summed[i:i + 1, :])


def write_kernel(dims, q_ref, zs_ref, zt_ref, lcol_ref, icol_ref, out_ref, stage, sem):
    seqs, draft, depth, vocab = dims
    rows = seqs * draft
    vtiles = pl.cdiv(vocab, LANES)
    first_tail = 2 * stream_trips(vocab) * BLOCK
    group = 32
    per = group // draft

    def copy(b, row):
        return pltpu.make_async_copy(stage.at[pl.ds(row, draft), :], out_ref.at[b], sem.at[b])

    @pl.loop(0, rows // group)
    def _(i):
        base = pl.multiple_of(i * group, group)
        r = pl.ds(base, group)
        inv = icol_ref[r, :]
        lr = lcol_ref[r, :]
        for v in range(vtiles):
            size = min(LANES, vocab - v * LANES)
            off = v * LANES - first_tail
            s = zs_ref[r, BLOCK + v * LANES:BLOCK + (v + 1) * LANES] if off < 0 else zt_ref[r, off:off + LANES]
            e = jnp.maximum(jnp.exp2(s - lr)[:, :size] - q_ref[r, v * LANES:v * LANES + size], 0.0)
            stage[r, v * LANES:v * LANES + size] = e * inv[:, :size]
        for b in range(per):
            copy(i * per + b, base + b * draft).start()

    for b in range(seqs):
        copy(b, b * draft).wait()


def solution(mesh):
    n = mesh.shape["tp"]

    def local_step(hidden, norm_gain, w_head, draft_probs, draft_tokens, temperature):
        seqs, draft, vocab = draft_probs.shape
        depth = w_head.shape[0]
        dims = (seqs, draft, depth, vocab)
        rows = seqs * draft
        total = rows + seqs
        me = lax.axis_index("tp")

        inv_t = LOG2E / temperature
        tok = (draft_tokens - me * vocab).astype(F32).reshape(rows)
        meta = jnp.concatenate([jnp.repeat(inv_t, draft), inv_t, jnp.zeros((LANES - seqs,), F32), tok,
                                jnp.zeros((3 * LANES,), F32)]).reshape(8, LANES)
        vmem = pl.BlockSpec(memory_space=pltpu.VMEM)
        hbm = pl.BlockSpec(memory_space=pl.ANY)
        ttail = vocab - 2 * stream_trips(vocab) * BLOCK
        zwide = (2 * stream_trips(vocab) + 1) * BLOCK
        streamed = pl.pallas_call(
            functools.partial(stream_kernel, dims),
            out_shape=(pltpu.VMEM((rows, vocab), F32), pltpu.VMEM((rows, zwide), F32),
                       pltpu.VMEM((total, depth), BF16), pltpu.VMEM((ttail, depth), BF16),
                       pltpu.VMEM((3 * LANES, LANES), F32), pltpu.VMEM((3 * LANES, LANES), F32),
                       pltpu.VMEM((rows, LANES), F32), pltpu.VMEM((rows, LANES), F32),
                       pltpu.VMEM((total, LANES), F32)),
            in_specs=[hbm, vmem, hbm, hbm, vmem],
            out_specs=(vmem,) * 9,
            scratch_shapes=[
                pltpu.VMEM((draft + 1, seqs, depth), BF16),
                pltpu.VMEM((2, total, LANES), F32),
                pltpu.VMEM((SLOTS, BLOCK, depth), BF16),
                pltpu.SemaphoreType.DMA,
                pltpu.SemaphoreType.DMA((SLOTS,)),
                pltpu.SemaphoreType.DMA((seqs,)),
                pltpu.SemaphoreType.DMA,
            ],
            compiler_params=pltpu.CompilerParams(vmem_limit_bytes=30 * 1024 * 1024),
            name="verify_stream",
        )(jnp.transpose(hidden, (1, 0, 2)), norm_gain.reshape(1, depth), w_head.T, draft_probs, meta)

        streamed = [pltpu.with_memory_space_constraint(x, pltpu.VMEM) for x in streamed]
        twide = pl.cdiv(ttail, LANES) * LANES
        shared = pl.pallas_call(
            functools.partial(exchange_kernel, dims, n),
            out_shape=(pltpu.VMEM((total, twide), F32), pltpu.VMEM((rows, LANES), F32),
                       jax.ShapeDtypeStruct((8, LANES), F32), pltpu.VMEM((rows, LANES), F32)),
            in_specs=[vmem] * 10,
            out_specs=(vmem,) * 4,
            scratch_shapes=[
                pltpu.VMEM((3 * LANES, LANES), F32),
                pltpu.VMEM((3 * LANES, LANES), F32),
                pltpu.VMEM((rows, LANES), F32),
                pltpu.VMEM((rows, LANES), F32),
                pltpu.VMEM((4, LANES), F32),
                pltpu.VMEM((n, 4, LANES), F32),
                pltpu.VMEM((4, LANES), F32),
                pltpu.VMEM((n, 4, LANES), F32),
                pltpu.SemaphoreType.DMA((n,)),
                pltpu.SemaphoreType.DMA((n,)),
                pltpu.SemaphoreType.DMA((n,)),
                pltpu.SemaphoreType.DMA((n,)),
            ],
            compiler_params=pltpu.CompilerParams(
                collective_id=0, has_side_effects=True, vmem_limit_bytes=6 * 1024 * 1024),
            name="verify_exchange",
        )(*streamed, meta)
        zt, lcol, stat, icol = shared

        residual = pl.pallas_call(
            functools.partial(write_kernel, dims),
            out_shape=jax.ShapeDtypeStruct((seqs, draft, vocab), F32),
            in_specs=[vmem] * 5,
            out_specs=hbm,
            scratch_shapes=[pltpu.VMEM((rows, vocab), F32), pltpu.SemaphoreType.DMA((seqs,))],
            compiler_params=pltpu.CompilerParams(vmem_limit_bytes=10 * 1024 * 1024),
            name="verify_write",
        )(streamed[0], streamed[1], *[pltpu.with_memory_space_constraint(x, pltpu.VMEM) for x in (zt, lcol, icol)])

        norm_sum = stat[0:2].reshape(seqs, draft)
        accept = stat[2:4].reshape(seqs, draft)
        bonus = stat[6, :seqs]
        return accept, norm_sum, residual, bonus

    return jax.shard_map(
        local_step,
        mesh=mesh,
        in_specs=(P('dp', None, None), P(), P(None, 'tp'), P('dp', None, 'tp'), P('dp', None), P('dp')),
        out_specs=(P('dp', None), P('dp', None), P('dp', None, 'tp'), P('dp')),
        check_vma=False,
    )
```

time: 183 us -> 60 us (0.33)
  blocking collectives: 94.6 us -> 0 us
  Pallas kernels: 0 us -> 54.6 us
  matrix products: 34.1 us -> 0 us
  other arithmetic: 31 us -> 1.35 us
  local copies, waits for them, and re-layouts: 21.5 us -> 3.08 us
    psum x2 -> x0, blocking collectives: 59.6 us -> none  [local_step(): lax.psum((local_sum, tok_scaled, tok_draft), 'tp')]
    pallas_call x0 -> x3, Pallas kernels: none -> 54.6 us  [the longest x1 33.7 us: local_step(): pl.pallas_call(functools.partial(stream_kernel, dims), out_shape=(pltpu.V...]
    pmax x1 -> x0, blocking collectives: 35 us -> none  [local_step(): row_max = lax.pmax(jnp.max(scaled, axis=-1), 'tp')]
    dot_general x1 -> x0, matrix products: 34.1 us -> none  [local_step(): jnp.einsum('cle,ew->clw', normed, w_head, preferred_element_type=jnp.floa...]
    reduce_sum x3 -> x0, other arithmetic: 20.4 us -> none  [the longest x1 12.7 us: local_step(): norm_sum = lax.psum(jnp.sum(excess, axis=-1), 'tp')]
    unnamed x11 -> x4, local copies, waits for them, and re-layouts: 12 us -> 1.31 us
    gather x8 -> x0, local copies, waits for them, and re-layouts: 8.95 us -> none  [the longest x5 4.68 us: local_step(): jnp.take_along_axis(scaled[:, :draft_len], safe_idx, axis=-1)[:, :, 0]]
    div x1, other arithmetic: 9.26 us -> 0.66 us  [local_step(): inv_t = LOG2E / temperature]
where the time goes in v1:
time: 60 us; the launch traced here: 59.8 us
  Pallas kernels  54.6 us (91%)
  local copies, waits for them, and re-layouts  3.08 us (5%)
  other arithmetic  1.35 us (2%)
  between operations  0.71 us (1%)
    pallas_call x1, Pallas kernels, local_step(): pl.pallas_call(functools.partial(stream_kernel, dims), out_shape=(pltpu.V...  33.7 us
    pallas_call x1, Pallas kernels, local_step(): pl.pallas_call(functools.partial(exchange_kernel, dims, n), out_shape=(pl...  16.9 us
    pallas_call x1, Pallas kernels, local_step(): pl.pallas_call(functools.partial(write_kernel, dims), out_shape=jax.Shape...  3.97 us
    unnamed x4, local copies, waits for them, and re-layouts  1.31 us

profile of v1, /device:TPU:0, one launch (start us, length us, event | category | flops | bytes accessed | tf_op | source)
XLA Modules:
  0.0 59.8 jit_solution(3490105414423655504)
XLA Ops:
  0.6 0.7 %broadcast_divide_fusion = f32[64]{0:T(128)S(1)} fusion(f32[64]{0:T(128)} %param.11), kind=kLoop, calls=%fused_computation.2 | loop fusion | flops 64 | bytes 512 | tf_op jit(solution)/shard_map/div | solution.py:392
  1.3 0.7 %subtract_convert_fusion = f32[64,4]{0,1:T(4,128)S(1)} fusion(s32[64,4]{0,1:T(4,128)} %param.10, s32[]{:T(128)S(6)} %mul.3), kind=kLoop, calls=%fused_computation | loop fusion | flops 512 | bytes 2052 | tf_op jit(solution)/shard_map/convert_element_type | solution.py:393
  2.0 0.1 copy.12
  2.1 0.1 reshape.28
  2.2 0.1 broadcast_in_dim.9
  2.3 0.1 reshape.27
  2.4 0.7 %concatenate.3 = f32[1024]{0:T(1024)} concatenate(f32[256]{0:T(256)S(1)} %reshape.27, f32[64]{0:T(128)S(1)} %broadcast_divide_fusion, f32[64]{0:T(128)S(1)} %broadcast_in_dim.10, f32[256]{0:T(256)S(1)} %reshape.28, f32[384]{0:T(512)S(1)} %broadcast_in_dim.11), dimensions={0} | concatenate | bytes 8192 | tf_op jit(solution)/shard_map/concatenate | solution.py:394
  3.1 0.0 copy-start
  3.1 33.7 %verify_stream.1 = (f32[256,8016]{1,0:T(8,128)S(1)}, f32[256,7680]{1,0:T(8,128)S(1)}, bf16[320,4096]{1,0:T(8,128)(2,1)S(1)}, bf16[848,4096]{1,0:T(8,128)(2,1)S(1...) custom-call(bf16[5,64,4096]{2,1,0:T(8,128)(2,1)} %bitcast.9, ...), custom_call_target="tpu_custom_call" | custom-call | tf_op jit(solution)/shard_map/verify_stream/pallas_call | solution.py:400
  36.8 0.0 copy-done
  36.8 16.9 %verify_exchange.1 = (f32[320,896]{1,0:T(8,128)S(1)}, f32[256,128]{1,0:T(8,128)S(1)}, f32[8,128]{1,0:T(8,128)S(1)}, f32[256,128]{1,0:T(8,128)S(1)}) custom-call(f32[256,8016]{1,0:T(8,128)S(1)} %get-tuple-element.17.q_ref, f32[256,7680]{1,0:T(8,128)S(1)} %get-tuple-element.18.zs_ref, bf16[320,4096]{1,0:T(8,128)(2,1)S(1)} %get-tuple-element.19.xb_ref, ...), custom_call_target="tpu_custom_call" | custom-call | tf_op jit(solution)/shard_map/verify_exchange/pallas_call | solution.py:424
  53.8 4.0 %verify_write.1 = f32[64,4,8016]{2,1,0:T(4,128)} custom-call(f32[256,8016]{1,0:T(8,128)S(1)} %get-tuple-element.17.q_ref, f32[256,7680]{1,0:T(8,128)S(1)} %get-tuple-element.18.zs_ref, f32[320,896]{1,0:T(8,128)S(1)} %get-tuple-element.27.zt_ref, f32[256,128]{1,0:T(8,128)S(1)} %get-tuple-element.28.lcol_ref, f32[256,128]{1,0:T(8,128)S(1)} %get-tuple-element.29.icol_ref), custom_call_target="tpu_custom_call" | custom-call | tf_op jit(solution)/shard_map/verify_write/pallas_call | solution.py:450
  57.7 0.5 slice_bitcast_fusion
  58.3 0.1 reshape.31
  58.4 0.7 %copy.14 = f32[64,4]{0,1:T(4,128)} copy(f32[64,4]{1,0:T(8,128)S(1)} %reshape.31) | data formatting | bytes 2048
  59.0 0.1 reshape.30
  59.1 0.7 %copy.13 = f32[64,4]{0,1:T(4,128)} copy(f32[64,4]{1,0:T(8,128)S(1)} %reshape.30) | data formatting | bytes 2048
  (3 shorter events, 0.0 us)
Async XLA Ops:
  3.1 33.7 %copy-start = (f32[1024]{0:T(1024)S(1)}, f32[1024]{0:T(1024)}, u32[]{:S(2)}) copy-start(f32[1024]{0:T(1024)} %concatenate.3) | copy-start | bytes 12292

commit v2 on v1

v2 whole, which is shorter than its diff:
```python
import functools

import jax
import jax.numpy as jnp
from jax import lax
from jax.experimental import pallas as pl
from jax.experimental.pallas import tpu as pltpu
from jax.sharding import PartitionSpec as P

MESH = pl.DeviceIdType.MESH
F32 = jnp.float32
BF16 = jnp.bfloat16
LOG2E = 1.4426950408889634
LN2 = 0.6931471805599453
NEG = -1e30
LANES = 128
TILE = 256
BLOCK = 2 * TILE
SLOTS = 6
PIECE = 64


def stream_blocks(vocab):
    return 2 * (vocab // (2 * BLOCK))


def column(row):
    return jnp.transpose(jnp.broadcast_to(row, (LANES, LANES)))


def stream_kernel(dims, hid_ref, gain_ref, wt_ref, temp_ref, tok_ref,
                  zs, xb, wtail, mx, sm, tokc, invc,
                  hid, xs, ring, row, hid_sem, w_sem, t_sem):
    seqs, draft, depth, vocab = dims
    rows = seqs * draft
    total = rows + seqs
    ktiles = depth // TILE
    nblocks = stream_blocks(vocab)
    tail = vocab - nblocks * BLOCK
    pieces = total // PIECE
    chunks = depth // LANES

    def w_copy(block):
        slot = lax.rem(block, SLOTS)
        return pltpu.make_async_copy(
            wt_ref.at[pl.ds(pl.multiple_of(block * BLOCK, BLOCK), BLOCK), :], ring.at[slot], w_sem.at[slot])

    tail_copy = pltpu.make_async_copy(wt_ref.at[pl.ds(nblocks * BLOCK, tail), :], wtail, t_sem)
    hid_copies = [pltpu.make_async_copy(hid_ref.at[j], hid.at[j], hid_sem.at[j]) for j in range(draft + 1)]
    for c in hid_copies:
        c.start()
    for i in range(SLOTS):
        w_copy(i).start(priority=1)

    mx[...] = jnp.full(mx.shape, NEG, F32)
    sm[...] = jnp.ones(sm.shape, F32)
    row[...] = jnp.ones(row.shape, F32)
    row[0:1, 0:seqs] = temp_ref[...]
    row[1:1 + draft, 0:seqs] = (tok_ref[...] - lax.axis_index("tp") * vocab).astype(F32)
    inv = LOG2E / column(row[0:1, :])[0:seqs, :]
    for j in range(draft):
        invc[pl.ds(j, seqs, stride=draft), :] = inv
        tokc[pl.ds(j, seqs, stride=draft), :] = column(row[1 + j:2 + j, :])[0:seqs, :]
    invc[pl.ds(rows, seqs), :] = inv

    invr = []
    for j in range(draft + 1):
        hid_copies[j].wait()

        def squares(c, acc, j=j):
            out = []
            for u in range(4):
                h = hid[j, :, pl.ds(pl.multiple_of((c * 4 + u) * LANES, LANES), LANES)].astype(F32)
                out.append(h * h)
            return acc + ((out[0] + out[1]) + (out[2] + out[3]))

        s = lax.fori_loop(0, chunks // 4, squares, jnp.zeros((seqs, LANES), F32))
        r = lax.rsqrt(jnp.sum(s, axis=-1, keepdims=True) * (1.0 / depth) + 1e-5)
        invr.append(jnp.broadcast_to(r, (seqs, LANES)))

    def normalise(c, carry):
        for u in range(2):
            lanes = pl.ds(pl.multiple_of((c * 2 + u) * LANES, LANES), LANES)
            g = gain_ref[:, lanes]
            for j in range(draft + 1):
                x = hid[j, :, lanes].astype(F32) * carry[j] * g
                if j < draft:
                    xs[u, pl.ds(j, seqs, stride=draft), :] = x
                else:
                    xb[pl.ds(rows, seqs), lanes] = x.astype(BF16)
        for u in range(2):
            lanes = pl.ds(pl.multiple_of((c * 2 + u) * LANES, LANES), LANES)
            xb[pl.ds(0, rows), lanes] = xs[u].astype(BF16)
        return carry

    lax.fori_loop(0, chunks // 2, normalise, tuple(invr))

    def stream(*accs):
        acc = [[accs[(par * 2 + q) * pieces:(par * 2 + q + 1) * pieces] for q in range(2)] for par in range(2)]

        def push(slot, k, q):
            pltpu.matmul_push_rhs(ring[slot, q * TILE:(q + 1) * TILE, k * TILE:(k + 1) * TILE],
                                  staging_register=k % 2, mxu_index=q, transpose=True)

        def process(par, block):
            for p in range(pieces):
                z = [pltpu.matmul_pop(acc[par][q][p]) for q in range(2)]
                r = pl.ds(p * PIECE, PIECE)
                inv = invc[r, :]
                s = [z[g // 2][:, (g % 2) * LANES:(g % 2 + 1) * LANES] * inv for g in range(4)]
                if (p + 1) * PIECE <= rows:
                    for g in range(4):
                        zs[r, pl.ds(pl.multiple_of(block * BLOCK + g * LANES, LANES), LANES)] = s[g]
                m_old = mx[r, :]
                m_new = jnp.maximum(jnp.maximum(m_old, jnp.maximum(s[0], s[1])), jnp.maximum(s[2], s[3]))
                e = sm[r, :] * jnp.exp2(m_old - m_new)
                e = e + ((jnp.exp2(s[0] - m_new) + jnp.exp2(s[1] - m_new))
                         + (jnp.exp2(s[2] - m_new) + jnp.exp2(s[3] - m_new)))
                mx[r, :] = m_new
                sm[r, :] = e

        def half(block, par, first=False, last=False, fetch=False):
            slot = lax.rem(block, SLOTS)
            after = lax.rem(block + 1, SLOTS)
            if not last:
                w_copy(block + 1).wait()
            if fetch:
                w_copy(block - 1 + SLOTS).start(priority=1)
            for k in range(ktiles):
                for q in range(2):
                    if k + 1 < ktiles:
                        push(slot, k + 1, q)
                    elif not last:
                        push(after, 0, q)
                for p in range(pieces):
                    x = xb[p * PIECE:(p + 1) * PIECE, k * TILE:(k + 1) * TILE]
                    for q in range(2):
                        pltpu.matmul_acc_lhs(acc[par][q][p], x, load_staged_rhs=(k % 2) if p == 0 else None)
                if k == 1 and not first:
                    process(1 - par, block - 1)

        for a in accs:
            pltpu.matmul_pop(a)
        w_copy(0).wait()
        for q in range(2):
            push(0, 0, q)
        half(0, 0, first=True)
        steady = (nblocks - SLOTS) // 2

        @pl.loop(0, steady)
        def _(trip):
            half(trip * 2 + 1, 1, fetch=True)
            half(trip * 2 + 2, 0, fetch=True)

        tail_copy.start(priority=1)

        @pl.loop(steady, (nblocks - 2) // 2)
        def _(trip):
            half(trip * 2 + 1, 1)
            half(trip * 2 + 2, 0)

        half(nblocks - 1, 1, last=True)
        process(1, nblocks - 1)

    pl.run_scoped(stream, *[pltpu.ACC(q)((PIECE, TILE), F32)
                            for _ in range(2) for q in range(2) for _ in range(pieces)])
    tail_copy.wait()


def exchange_kernel(dims, n, q_hbm, zs_ref, xb_ref, wtail_ref, mx_ref, sm_ref, tokc_ref, invc_ref, tok_ref,
                    q_ref, zt, lcol, icol, stat,
                    mx, sm, ta, tb, own, send1, recv1, send2, recv2, q_sem, s1_sem, r1_sem, s2_sem, r2_sem):
    seqs, draft, depth, vocab = dims
    rows = seqs * draft
    total = rows + seqs
    me = lax.axis_index("tp")
    first_tail = stream_blocks(vocab) * BLOCK
    tail = vocab - first_tail
    vtiles = pl.cdiv(vocab, LANES)
    ttiles = pl.cdiv(tail, LANES)
    lane = lax.broadcasted_iota(jnp.int32, (8, LANES), 1)
    half = seqs

    barrier = pltpu.get_barrier_semaphore()
    for d in range(1, n):
        pl.semaphore_signal(barrier, inc=1, device_id={"tp": lax.rem(me + d, n)}, device_id_type=MESH)

    q_copies = [pltpu.make_async_copy(q_hbm.at[b], q_ref.at[pl.ds(b * draft, draft), :], q_sem.at[b])
                for b in range(seqs)]
    for c in q_copies:
        c.start(priority=1)

    zt[:, :tail] = lax.dot_general(xb_ref[...], wtail_ref[...], (((1,), (1,)), ((), ())),
                                   preferred_element_type=F32)
    step = 32

    def finish(i, is_draft):
        r = pl.ds(pl.multiple_of(i * step, step), step)
        inv = invc_ref[r, :]
        s = []
        for g in range(ttiles):
            v = zt[r, g * LANES:(g + 1) * LANES] * inv
            if (g + 1) * LANES > tail:
                v = jnp.where(jnp.broadcast_to((lane + g * LANES < tail)[0:1], (step, LANES)), v, NEG)
            s.append(v)
        if is_draft:
            for g in range(ttiles):
                zt[r, g * LANES:(g + 1) * LANES] = s[g]
        m_old = mx_ref[r, :]
        m_new = functools.reduce(jnp.maximum, s, m_old)
        e = sm_ref[r, :] * jnp.exp2(m_old - m_new)
        for v in s:
            e = e + jnp.exp2(v - m_new)
        mx[r, :] = m_new
        sm[r, :] = e

    @pl.loop(0, rows // step)
    def _(i):
        finish(i, True)

    @pl.loop(rows // step, total // step)
    def _(i):
        finish(i, False)

    def rows_of(ref, j):
        return ref[pl.ds(j, seqs, stride=draft), :]

    for j in range(draft):
        mt = jnp.transpose(jnp.concatenate([rows_of(mx, j), mx[pl.ds(rows, seqs), :]], axis=0))
        st = jnp.transpose(jnp.concatenate([rows_of(sm, j), sm[pl.ds(rows, seqs), :]], axis=0))
        top = jnp.max(mt, axis=0, keepdims=True)
        tot = jnp.sum(st * jnp.exp2(mt - top), axis=0, keepdims=True)
        lse = top + jnp.log(tot) * LOG2E
        send1[j:j + 1, :] = lse
        recv1[me, j:j + 1, :] = lse

    pl.semaphore_wait(barrier, n - 1)

    def exchange(send, recv, s_sem, r_sem):
        return [pltpu.make_async_remote_copy(
            src_ref=send, dst_ref=recv.at[me], send_sem=s_sem.at[d], recv_sem=r_sem.at[d],
            device_id={"tp": lax.rem(me + d, n)}, device_id_type=MESH) for d in range(1, n)]

    first = exchange(send1, recv1, s1_sem, r1_sem)
    for c in first:
        c.start()

    own[...] = jnp.zeros(own.shape, jnp.int32)
    own[:, 0:seqs] = tok_ref[...] - me * vocab
    for c in q_copies:
        c.wait()

    group = 32

    def scaled(r, v):
        off = v * LANES - first_tail
        return zs_ref[r, v * LANES:(v + 1) * LANES] if off < 0 else zt[r, off:off + LANES]

    def gather(i, carry):
        r = pl.ds(pl.multiple_of(i * group, group), group)
        tokr = tokc_ref[r, :]
        acc_s = jnp.zeros((group, LANES), F32)
        acc_q = jnp.zeros((group, LANES), F32)
        for v in range(vtiles):
            size = min(LANES, vocab - v * LANES)
            hit = tokr == (lane + v * LANES).astype(F32)[0:1]
            acc_s = acc_s + jnp.where(hit, scaled(r, v), 0.0)
            if size == LANES:
                acc_q = acc_q + jnp.where(hit, q_ref[r, v * LANES:(v + 1) * LANES], 0.0)
            else:
                part = jnp.where(hit[:, :size], q_ref[r, v * LANES:v * LANES + size], 0.0)
                acc_q = acc_q + jnp.pad(part, ((0, 0), (0, LANES - size)))
        ta[r, :] = acc_s
        tb[r, :] = acc_q
        return carry

    lax.fori_loop(0, rows // group, gather, 0)
    picked = [jnp.sum(jnp.transpose(jnp.concatenate([rows_of(ta, j), rows_of(tb, j)], axis=0)),
                      axis=0, keepdims=True) for j in range(draft)]

    for c in first:
        c.wait()

    parts = [recv1[i] for i in range(n)]
    top = functools.reduce(jnp.maximum, parts)
    tot = functools.reduce(jnp.add, [jnp.exp2(x - top) for x in parts])
    full = top + jnp.log(tot) * LOG2E
    for j in range(draft):
        lcol[pl.ds(j, seqs, stride=draft), :] = column(full[j:j + 1, :])[0:seqs, :]

    def excess(i, carry):
        r = pl.ds(pl.multiple_of(i * group, group), group)
        lr = lcol[r, :]
        acc = jnp.zeros((group, LANES), F32)
        for v in range(vtiles):
            size = min(LANES, vocab - v * LANES)
            e = jnp.maximum(jnp.exp2(scaled(r, v) - lr)[:, :size] - q_ref[r, v * LANES:v * LANES + size], 0.0)
            acc = acc + (e if size == LANES else jnp.pad(e, ((0, 0), (0, LANES - size))))
        ta[r, :] = acc
        return carry

    lax.fori_loop(0, rows // group, excess, 0)

    for j in range(draft):
        part = jnp.sum(jnp.transpose(jnp.concatenate([rows_of(ta, j), rows_of(ta, j)], axis=0)),
                       axis=0, keepdims=True)
        tok = own[j:j + 1, :]
        owned = (tok >= 0) & (tok < vocab)
        ratio = jnp.minimum(1.0, jnp.exp2(picked[j] - full[j:j + 1, :])
                            / jnp.where(owned, pltpu.roll(picked[j], half, 1), 1.0))
        ratio = jnp.where(owned, ratio, 0.0)
        both = jnp.where(lane[0:1] < half, part, pltpu.roll(ratio, half, 1))
        send2[j:j + 1, :] = both
        recv2[me, j:j + 1, :] = both

    second = exchange(send2, recv2, s2_sem, r2_sem)
    for c in second:
        c.start()
    for c in second:
        c.wait()
    summed = functools.reduce(jnp.add, [recv2[i] for i in range(n)])
    stat[0:4, :] = summed
    stat[4:8, :] = pltpu.roll(full * LN2, half, 1)
    for j in range(draft):
        icol[pl.ds(j, seqs, stride=draft), :] = column(1.0 / summed[j:j + 1, :])[0:seqs, :]


def write_kernel(dims, q_ref, zs_ref, zt_ref, lcol_ref, icol_ref, stat_ref,
                 out_ref, accept_ref, norm_ref, bonus_ref, stage, sem):
    seqs, draft, depth, vocab = dims
    rows = seqs * draft
    vtiles = pl.cdiv(vocab, LANES)
    first_tail = stream_blocks(vocab) * BLOCK
    group = 32
    per = group // draft

    def copy(b, row):
        return pltpu.make_async_copy(stage.at[pl.ds(row, draft), :], out_ref.at[b], sem.at[b])

    @pl.loop(0, rows // group)
    def _(i):
        base = pl.multiple_of(i * group, group)
        r = pl.ds(base, group)
        inv = icol_ref[r, :]
        lr = lcol_ref[r, :]
        for v in range(vtiles):
            size = min(LANES, vocab - v * LANES)
            off = v * LANES - first_tail
            s = zs_ref[r, v * LANES:(v + 1) * LANES] if off < 0 else zt_ref[r, off:off + LANES]
            e = jnp.maximum(jnp.exp2(s - lr)[:, :size] - q_ref[r, v * LANES:v * LANES + size], 0.0)
            stage[r, v * LANES:v * LANES + size] = e * inv[:, :size]
        for b in range(per):
            copy(i * per + b, base + b * draft).start(priority=1)

    norm_ref[...] = stat_ref[0:draft, 0:seqs]
    accept_ref[...] = pltpu.roll(stat_ref[0:draft, :], seqs, 1)[:, 0:seqs]
    bonus_ref[...] = stat_ref[4:5, 0:seqs]
    for b in range(seqs):
        copy(b, b * draft).wait()


def solution(mesh):
    n = mesh.shape["tp"]

    def local_step(hidden, norm_gain, w_head, draft_probs, draft_tokens, temperature):
        seqs, draft, vocab = draft_probs.shape
        depth = w_head.shape[0]
        dims = (seqs, draft, depth, vocab)
        rows = seqs * draft
        total = rows + seqs
        zwide = stream_blocks(vocab) * BLOCK
        ttail = vocab - zwide
        twide = pl.cdiv(ttail, LANES) * LANES
        vmem = pl.BlockSpec(memory_space=pltpu.VMEM)
        hbm = pl.BlockSpec(memory_space=pl.ANY)

        def held(xs):
            return [pltpu.with_memory_space_constraint(x, pltpu.VMEM) for x in xs]

        tokens = draft_tokens.T
        streamed = pl.pallas_call(
            functools.partial(stream_kernel, dims),
            out_shape=(pltpu.VMEM((rows, zwide), F32),
                       pltpu.VMEM((total, depth), BF16), pltpu.VMEM((ttail, depth), BF16),
                       pltpu.VMEM((total, LANES), F32), pltpu.VMEM((total, LANES), F32),
                       pltpu.VMEM((rows, LANES), F32), pltpu.VMEM((total, LANES), F32)),
            in_specs=[hbm, vmem, hbm, vmem, vmem],
            out_specs=(vmem,) * 7,
            scratch_shapes=[
                pltpu.VMEM((draft + 1, seqs, depth), BF16),
                pltpu.VMEM((2, rows, LANES), F32),
                pltpu.VMEM((SLOTS, BLOCK, depth), BF16),
                pltpu.VMEM((8, LANES), F32),
                pltpu.SemaphoreType.DMA((draft + 1,)),
                pltpu.SemaphoreType.DMA((SLOTS,)),
                pltpu.SemaphoreType.DMA,
            ],
            compiler_params=pltpu.CompilerParams(vmem_limit_bytes=30 * 1024 * 1024),
            name="verify_stream",
        )(pltpu.with_memory_space_constraint(jnp.transpose(hidden, (1, 0, 2)), pltpu.HBM), norm_gain.reshape(1, depth), w_head.T,
          temperature.reshape(1, seqs), tokens)
        zs = streamed[0]

        shared = pl.pallas_call(
            functools.partial(exchange_kernel, dims, n),
            out_shape=(pltpu.VMEM((rows, vocab), F32), pltpu.VMEM((total, twide), F32),
                       pltpu.VMEM((rows, LANES), F32), pltpu.VMEM((rows, LANES), F32),
                       pltpu.VMEM((8, LANES), F32)),
            in_specs=[hbm] + [vmem] * 8,
            out_specs=(vmem,) * 5,
            scratch_shapes=[
                pltpu.VMEM((total, LANES), F32),
                pltpu.VMEM((total, LANES), F32),
                pltpu.VMEM((rows, LANES), F32),
                pltpu.VMEM((rows, LANES), F32),
                pltpu.VMEM((draft, LANES), jnp.int32),
                pltpu.VMEM((4, LANES), F32),
                pltpu.VMEM((n, 4, LANES), F32),
                pltpu.VMEM((4, LANES), F32),
                pltpu.VMEM((n, 4, LANES), F32),
                pltpu.SemaphoreType.DMA((seqs,)),
                pltpu.SemaphoreType.DMA((n,)),
                pltpu.SemaphoreType.DMA((n,)),
                pltpu.SemaphoreType.DMA((n,)),
                pltpu.SemaphoreType.DMA((n,)),
            ],
            compiler_params=pltpu.CompilerParams(
                collective_id=0, has_side_effects=True, vmem_limit_bytes=6 * 1024 * 1024),
            name="verify_exchange",
        )(pltpu.with_memory_space_constraint(draft_probs, pltpu.HBM), *held(streamed), tokens)

        residual, accept, norm_sum, bonus = pl.pallas_call(
            functools.partial(write_kernel, dims),
            out_shape=(jax.ShapeDtypeStruct((seqs, draft, vocab), F32),
                       jax.ShapeDtypeStruct((draft, seqs), F32), jax.ShapeDtypeStruct((draft, seqs), F32),
                       jax.ShapeDtypeStruct((1, seqs), F32)),
            in_specs=[vmem] * 6,
            out_specs=(hbm, vmem, vmem, vmem),
            scratch_shapes=[pltpu.VMEM((rows, vocab), F32), pltpu.SemaphoreType.DMA((seqs,))],
            compiler_params=pltpu.CompilerParams(vmem_limit_bytes=10 * 1024 * 1024),
            name="verify_write",
        )(*held((shared[0], zs) + tuple(shared[1:])))

        return accept.T, norm_sum.T, residual, bonus.reshape(seqs)

    return jax.shard_map(
        local_step,
        mesh=mesh,
        in_specs=(P('dp', None, None), P(), P(None, 'tp'), P('dp', None, 'tp'), P('dp', None), P('dp')),
        out_specs=(P('dp', None), P('dp', None), P('dp', None, 'tp'), P('dp')),
        check_vma=False,
    )
```

time: 60 us -> 51.5 us (0.86)
  Pallas kernels: 54.6 us -> 48.6 us
  other arithmetic: 1.35 us -> 0 us
  local copies, waits for them, and re-layouts: 3.08 us -> 2.05 us
    pallas_call x1, Pallas kernels: 33.7 us -> 24.5 us  [local_step(): pl.pallas_call(functools.partial(stream_kernel, dims), out_shape=(pltpu.V...]
    pallas_call x1, Pallas kernels: 16.9 us -> 19.5 us  [local_step(): pl.pallas_call(functools.partial(exchange_kernel, dims, n), out_shape=(pl...]
    unnamed x4 -> x6, local copies, waits for them, and re-layouts: 1.31 us -> 2.05 us
    convert_element_type x1 -> x0, other arithmetic: 0.69 us -> none  [local_step(): tok = (draft_tokens - me * vocab).astype(F32).reshape(rows)]
    concatenate x1 -> x0, local copies, waits for them, and re-layouts: 0.66 us -> none  [local_step(): jnp.concatenate([jnp.repeat(inv_t, draft), inv_t, jnp.zeros((LANES - seqs...]
    div x1 -> x0, other arithmetic: 0.66 us -> none  [local_step(): inv_t = LOG2E / temperature]
where the time goes in v2:
time: 51.5 us; the launch traced here: 51.3 us
  Pallas kernels  48.6 us (94%)
  local copies, waits for them, and re-layouts  2.05 us (4%)
  between operations  0.66 us (1%)
    pallas_call x1, Pallas kernels, local_step(): pl.pallas_call(functools.partial(stream_kernel, dims), out_shape=(pltpu.V...  24.5 us
    pallas_call x1, Pallas kernels, local_step(): pl.pallas_call(functools.partial(exchange_kernel, dims, n), out_shape=(pl...  19.5 us
    pallas_call x1, Pallas kernels, local_step(): pl.pallas_call(functools.partial(write_kernel, dims), out_shape=(jax.Shap...  4.54 us
    unnamed x6, local copies, waits for them, and re-layouts  2.05 us

profile of v2, /device:TPU:0, one launch (start us, length us, event | category | flops | bytes accessed | tf_op | source)
XLA Modules:
  0.0 51.3 jit_solution(8306332560740052521)
XLA Ops:
  0.6 0.0 copy-start
  0.6 0.7 %copy-done = f32[4096]{0:T(1024)S(1)} copy-done((f32[4096]{0:T(1024)S(1)}, f32[4096]{0:T(1024)}, u32[]{:S(2)}) %copy-start) | copy-done | bytes 16408
  1.4 0.0 copy-start.1
  1.4 0.7 %copy-done.1 = s32[64,4]{0,1:T(4,128)S(1)} copy-done((s32[64,4]{0,1:T(4,128)S(1)}, s32[64,4]{0,1:T(4,128)}, u32[]{:S(2)}) %copy-start.1) | copy-done | bytes 1048
  2.0 0.0 copy-start.2
  2.0 0.7 %copy-done.2 = f32[64]{0:T(128)S(1)} copy-done((f32[64]{0:T(128)S(1)}, f32[64]{0:T(128)}, u32[]{:S(2)}) %copy-start.2) | copy-done | bytes 280
  2.7 24.5 %verify_stream.1 = (f32[256,7168]{1,0:T(8,128)S(1)}, bf16[320,4096]{1,0:T(8,128)(2,1)S(1)}, bf16[848,4096]{1,0:T(8,128)(2,1)S(1)}, f32[320,128]{1,0:T(8,128)S(1)...) custom-call(bf16[5,64,4096]{2,1,0:T(8,128)(2,1)} %bitcast.13, f32[1,4096]{1,0:T(1,128)S(1)} %bitcast.8, ...), custom_call_target="tpu_custom_call" | custom-call | tf_op jit(solution)/shard_map/verify_stream/pallas_call | solution.py:381
  27.2 19.5 %verify_exchange.1 = (f32[256,8016]{1,0:T(8,128)S(1)}, f32[320,896]{1,0:T(8,128)S(1)}, f32[256,128]{1,0:T(8,128)S(1)}, f32[256,128]{1,0:T(8,128)S(1)}, f32[8,128]{1,0:T(8,128)S(1)}) custom-call(f32[64,4,8016]{2,1,0:T(4,128)} %q_hbm.1, f32[256,7168]{1,0:T(8,128)S(1)} %get-tuple-element.20.zs_ref, bf16[320,4096]{1,0:T(8,128)(2,1)S(1)} %get-tuple-element.21.xb_ref, ...), custom_call_target="tpu_custom_call" | custom-call | tf_op jit(solution)/shard_map/verify_exchange/pallas_call | solution.py:404
  46.7 4.5 %verify_write.1 = (f32[64,4,8016]{2,1,0:T(4,128)}, f32[4,64]{1,0:T(4,128)}, f32[4,64]{1,0:T(4,128)}, f32[1,64]{1,0:T(1,128)}) custom-call(f32[256,8016]{1,0:T(8,128)S(1)} %get-tuple-element.27.q_ref, f32[256,7168]{1,0:T(8,128)S(1)} %get-tuple-element.20.zs_ref, f32[320,896]{1,0:T(8,128)S(1)} %get-tuple-element.28.zt_ref, ...), custom_call_target="tpu_custom_call" | custom-call | tf_op jit(solution)/shard_map/verify_write/pallas_call | solution.py:432
Async XLA Ops:
  0.6 0.7 %copy-start = (f32[4096]{0:T(1024)S(1)}, f32[4096]{0:T(1024)}, u32[]{:S(2)}) copy-start(f32[4096]{0:T(1024)} %param.7) | copy-start | bytes 49156
  1.4 0.7 %copy-start.1 = (s32[64,4]{0,1:T(4,128)S(1)}, s32[64,4]{0,1:T(4,128)}, u32[]{:S(2)}) copy-start(s32[64,4]{0,1:T(4,128)} %param.10) | copy-start | bytes 3076
  2.0 0.7 %copy-start.2 = (f32[64]{0:T(128)S(1)}, f32[64]{0:T(128)}, u32[]{:S(2)}) copy-start(f32[64]{0:T(128)} %param.11) | copy-start | bytes 772

commit v3 on v2

--- a/solution.py
+++ b/solution.py
@@ -28,9 +28,9 @@
     return jnp.transpose(jnp.broadcast_to(row, (LANES, LANES)))
 
 
-def stream_kernel(dims, hid_ref, gain_ref, wt_ref, temp_ref, tok_ref,
-                  zs, xb, wtail, mx, sm, tokc, invc,
-                  hid, xs, ring, row, hid_sem, w_sem, t_sem):
+def stream_kernel(dims, hid_hbm, gain_hbm, wt_ref, temp_hbm, tok_hbm,
+                  zs, xb, wtail, mx, sm, tokc, invc, own,
+                  hid, xs, ring, row, gain_ref, temp_ref, tok_ref, rr, hid_sem, w_sem, t_sem, c_sem, f_sem):
     seqs, draft, depth, vocab = dims
     rows = seqs * draft
     total = rows + seqs
@@ -46,54 +46,62 @@
             wt_ref.at[pl.ds(pl.multiple_of(block * BLOCK, BLOCK), BLOCK), :], ring.at[slot], w_sem.at[slot])
 
     tail_copy = pltpu.make_async_copy(wt_ref.at[pl.ds(nblocks * BLOCK, tail), :], wtail, t_sem)
-    hid_copies = [pltpu.make_async_copy(hid_ref.at[j], hid.at[j], hid_sem.at[j]) for j in range(draft + 1)]
-    for c in hid_copies:
+    hid_copies = [pltpu.make_async_copy(hid_hbm.at[j], hid.at[j], hid_sem.at[j]) for j in range(draft + 1)]
+    small = [pltpu.make_async_copy(a, b, c_sem.at[i]) for i, (a, b) in enumerate(
+        [(temp_hbm, temp_ref), (tok_hbm, tok_ref), (gain_hbm, gain_ref)])]
+    for c in small + hid_copies:
         c.start()
-    for i in range(SLOTS):
+    fold = depth // 2
+    first_copies = [pltpu.make_async_copy(
+        wt_ref.at[pl.ds(0, BLOCK), pl.ds(i * fold, fold)], ring.at[0, :, pl.ds(i * fold, fold)], f_sem.at[i])
+        for i in range(2)]
+    for c in first_copies:
+        c.start(priority=1)
+    for i in range(1, SLOTS):
         w_copy(i).start(priority=1)
 
     mx[...] = jnp.full(mx.shape, NEG, F32)
     sm[...] = jnp.ones(sm.shape, F32)
     row[...] = jnp.ones(row.shape, F32)
+    own[...] = jnp.zeros(own.shape, jnp.int32)
+    for c in small:
+        c.wait()
     row[0:1, 0:seqs] = temp_ref[...]
-    row[1:1 + draft, 0:seqs] = (tok_ref[...] - lax.axis_index("tp") * vocab).astype(F32)
+    own[:, 0:seqs] = tok_ref[...] - lax.axis_index("tp") * vocab
+    row[1:1 + draft, 0:seqs] = own[:, 0:seqs].astype(F32)
     inv = LOG2E / column(row[0:1, :])[0:seqs, :]
     for j in range(draft):
         invc[pl.ds(j, seqs, stride=draft), :] = inv
         tokc[pl.ds(j, seqs, stride=draft), :] = column(row[1 + j:2 + j, :])[0:seqs, :]
     invc[pl.ds(rows, seqs), :] = inv
 
-    invr = []
     for j in range(draft + 1):
         hid_copies[j].wait()
 
         def squares(c, acc, j=j):
-            out = []
-            for u in range(4):
-                h = hid[j, :, pl.ds(pl.multiple_of((c * 4 + u) * LANES, LANES), LANES)].astype(F32)
-                out.append(h * h)
-            return acc + ((out[0] + out[1]) + (out[2] + out[3]))
-
-        s = lax.fori_loop(0, chunks // 4, squares, jnp.zeros((seqs, LANES), F32))
+            for u in range(16):
+                h = hid[j, :, pl.ds(pl.multiple_of((c * 16 + u) * LANES, LANES), LANES)].astype(F32)
+                acc = acc + h * h
+            return acc
+
+        s = lax.fori_loop(0, chunks // 16, squares, jnp.zeros((seqs, LANES), F32))
         r = lax.rsqrt(jnp.sum(s, axis=-1, keepdims=True) * (1.0 / depth) + 1e-5)
-        invr.append(jnp.broadcast_to(r, (seqs, LANES)))
-
-    def normalise(c, carry):
+        rr[j] = jnp.broadcast_to(r, (seqs, LANES))
+
+    def normalise(k):
         for u in range(2):
-            lanes = pl.ds(pl.multiple_of((c * 2 + u) * LANES, LANES), LANES)
+            lanes = slice((k * 2 + u) * LANES, (k * 2 + u + 1) * LANES)
+            slab = (k * 2 + u) % 4
             g = gain_ref[:, lanes]
             for j in range(draft + 1):
-                x = hid[j, :, lanes].astype(F32) * carry[j] * g
+                x = hid[j, :, lanes].astype(F32) * rr[j] * g
                 if j < draft:
-                    xs[u, pl.ds(j, seqs, stride=draft), :] = x
+                    xs[slab, pl.ds(j, seqs, stride=draft), :] = x
                 else:
                     xb[pl.ds(rows, seqs), lanes] = x.astype(BF16)
-        for u in range(2):
-            lanes = pl.ds(pl.multiple_of((c * 2 + u) * LANES, LANES), LANES)
-            xb[pl.ds(0, rows), lanes] = xs[u].astype(BF16)
-        return carry
-
-    lax.fori_loop(0, chunks // 2, normalise, tuple(invr))
+            xb[pl.ds(0, rows), lanes] = xs[slab].astype(BF16)
+
+    normalise(0)
 
     def stream(*accs):
         acc = [[accs[(par * 2 + q) * pieces:(par * 2 + q + 1) * pieces] for q in range(2)] for par in range(2)]
@@ -102,8 +110,8 @@
             pltpu.matmul_push_rhs(ring[slot, q * TILE:(q + 1) * TILE, k * TILE:(k + 1) * TILE],
                                   staging_register=k % 2, mxu_index=q, transpose=True)
 
-        def process(par, block):
-            for p in range(pieces):
+        def process(par, block, which):
+            for p in which:
                 z = [pltpu.matmul_pop(acc[par][q][p]) for q in range(2)]
                 r = pl.ds(p * PIECE, PIECE)
                 inv = invc[r, :]
@@ -122,11 +130,16 @@
         def half(block, par, first=False, last=False, fetch=False):
             slot = lax.rem(block, SLOTS)
             after = lax.rem(block + 1, SLOTS)
-            if not last:
-                w_copy(block + 1).wait()
-            if fetch:
-                w_copy(block - 1 + SLOTS).start(priority=1)
             for k in range(ktiles):
+                if first and k == ktiles // 2 - 1:
+                    first_copies[1].wait()
+                if k == ktiles - 1:
+                    if not last:
+                        w_copy(block + 1).wait()
+                    if fetch:
+                        w_copy(block - 1 + SLOTS).start(priority=1)
+                if first and k + 1 < ktiles:
+                    normalise(k + 1)
                 for q in range(2):
                     if k + 1 < ktiles:
                         push(slot, k + 1, q)
@@ -136,12 +149,11 @@
                     x = xb[p * PIECE:(p + 1) * PIECE, k * TILE:(k + 1) * TILE]
                     for q in range(2):
                         pltpu.matmul_acc_lhs(acc[par][q][p], x, load_staged_rhs=(k % 2) if p == 0 else None)
-                if k == 1 and not first:
-                    process(1 - par, block - 1)
-
-        for a in accs:
-            pltpu.matmul_pop(a)
-        w_copy(0).wait()
+                if k % 2 == 1 and k // 2 < pieces and not first:
+                    process(1 - par, block - 1, [k // 2])
+
+        for c in first_copies[:1]:
+            c.wait()
         for q in range(2):
             push(0, 0, q)
         half(0, 0, first=True)
@@ -160,16 +172,16 @@
             half(trip * 2 + 2, 0)
 
         half(nblocks - 1, 1, last=True)
-        process(1, nblocks - 1)
+        process(1, nblocks - 1, range(pieces))
 
     pl.run_scoped(stream, *[pltpu.ACC(q)((PIECE, TILE), F32)
                             for _ in range(2) for q in range(2) for _ in range(pieces)])
     tail_copy.wait()
 
 
-def exchange_kernel(dims, n, q_hbm, zs_ref, xb_ref, wtail_ref, mx_ref, sm_ref, tokc_ref, invc_ref, tok_ref,
-                    q_ref, zt, lcol, icol, stat,
-                    mx, sm, ta, tb, own, send1, recv1, send2, recv2, q_sem, s1_sem, r1_sem, s2_sem, r2_sem):
+def exchange_kernel(dims, n, q_hbm, zs_ref, xb_ref, wtail_ref, mx_ref, sm_ref, tokc_ref, invc_ref, own,
+                    q_ref, icol, stat,
+                    zt, lcol, mx, sm, ta, tb, send1, recv1, send2, recv2, q_sem, s1_sem, r1_sem, s2_sem, r2_sem):
     seqs, draft, depth, vocab = dims
     rows = seqs * draft
     total = rows + seqs
@@ -245,8 +257,6 @@
     for c in first:
         c.start()
 
-    own[...] = jnp.zeros(own.shape, jnp.int32)
-    own[:, 0:seqs] = tok_ref[...] - me * vocab
     for c in q_copies:
         c.wait()
 
@@ -295,6 +305,7 @@
         for v in range(vtiles):
             size = min(LANES, vocab - v * LANES)
             e = jnp.maximum(jnp.exp2(scaled(r, v) - lr)[:, :size] - q_ref[r, v * LANES:v * LANES + size], 0.0)
+            q_ref[r, v * LANES:v * LANES + size] = e
             acc = acc + (e if size == LANES else jnp.pad(e, ((0, 0), (0, LANES - size))))
         ta[r, :] = acc
         return carry
@@ -325,14 +336,19 @@
         icol[pl.ds(j, seqs, stride=draft), :] = column(1.0 / summed[j:j + 1, :])[0:seqs, :]
 
 
-def write_kernel(dims, q_ref, zs_ref, zt_ref, lcol_ref, icol_ref, stat_ref,
-                 out_ref, accept_ref, norm_ref, bonus_ref, stage, sem):
+def write_kernel(dims, exc_ref, icol_ref, stat_ref,
+                 out_ref, accept_hbm, norm_hbm, bonus_hbm, accept_ref, norm_ref, bonus_ref, stage, sem, small_sem):
     seqs, draft, depth, vocab = dims
     rows = seqs * draft
     vtiles = pl.cdiv(vocab, LANES)
-    first_tail = stream_blocks(vocab) * BLOCK
-    group = 32
+    group = 16
     per = group // draft
+
+    norm_ref[...] = stat_ref[0:draft, 0:seqs]
+    accept_ref[...] = pltpu.roll(stat_ref[0:draft, :], seqs, 1)[:, 0:seqs]
+    bonus_ref[...] = stat_ref[4:5, 0:seqs]
+    small = [pltpu.make_async_copy(a, b, small_sem.at[i]) for i, (a, b) in enumerate(
+        [(accept_ref, accept_hbm), (norm_ref, norm_hbm), (bonus_ref, bonus_hbm)])]
 
     def copy(b, row):
         return pltpu.make_async_copy(stage.at[pl.ds(row, draft), :], out_ref.at[b], sem.at[b])
@@ -342,21 +358,18 @@
         base = pl.multiple_of(i * group, group)
         r = pl.ds(base, group)
         inv = icol_ref[r, :]
-        lr = lcol_ref[r, :]
         for v in range(vtiles):
             size = min(LANES, vocab - v * LANES)
-            off = v * LANES - first_tail
-            s = zs_ref[r, v * LANES:(v + 1) * LANES] if off < 0 else zt_ref[r, off:off + LANES]
-            e = jnp.maximum(jnp.exp2(s - lr)[:, :size] - q_ref[r, v * LANES:v * LANES + size], 0.0)
-            stage[r, v * LANES:v * LANES + size] = e * inv[:, :size]
+            stage[r, v * LANES:v * LANES + size] = exc_ref[r, v * LANES:v * LANES + size] * inv[:, :size]
         for b in range(per):
-            copy(i * per + b, base + b * draft).start(priority=1)
-
-    norm_ref[...] = stat_ref[0:draft, 0:seqs]
-    accept_ref[...] = pltpu.roll(stat_ref[0:draft, :], seqs, 1)[:, 0:seqs]
-    bonus_ref[...] = stat_ref[4:5, 0:seqs]
+            copy(i * per + b, base + b * draft).start(priority=b % 2)
+
+    for c in small:
+        c.start()
     for b in range(seqs):
         copy(b, b * draft).wait()
+    for c in small:
+        c.wait()
 
 
 def solution(mesh):
@@ -377,43 +390,49 @@
         def held(xs):
             return [pltpu.with_memory_space_constraint(x, pltpu.VMEM) for x in xs]
 
-        tokens = draft_tokens.T
         streamed = pl.pallas_call(
             functools.partial(stream_kernel, dims),
             out_shape=(pltpu.VMEM((rows, zwide), F32),
                        pltpu.VMEM((total, depth), BF16), pltpu.VMEM((ttail, depth), BF16),
                        pltpu.VMEM((total, LANES), F32), pltpu.VMEM((total, LANES), F32),
-                       pltpu.VMEM((rows, LANES), F32), pltpu.VMEM((total, LANES), F32)),
-            in_specs=[hbm, vmem, hbm, vmem, vmem],
-            out_specs=(vmem,) * 7,
+                       pltpu.VMEM((rows, LANES), F32), pltpu.VMEM((total, LANES), F32),
+                       pltpu.VMEM((draft, LANES), jnp.int32)),
+            in_specs=[hbm] * 5,
+            out_specs=(vmem,) * 8,
             scratch_shapes=[
                 pltpu.VMEM((draft + 1, seqs, depth), BF16),
-                pltpu.VMEM((2, rows, LANES), F32),
+                pltpu.VMEM((4, rows, LANES), F32),
                 pltpu.VMEM((SLOTS, BLOCK, depth), BF16),
                 pltpu.VMEM((8, LANES), F32),
+                pltpu.VMEM((1, depth), F32),
+                pltpu.VMEM((1, seqs), F32),
+                pltpu.VMEM((draft, seqs), jnp.int32),
+                pltpu.VMEM((draft + 1, seqs, LANES), F32),
                 pltpu.SemaphoreType.DMA((draft + 1,)),
                 pltpu.SemaphoreType.DMA((SLOTS,)),
                 pltpu.SemaphoreType.DMA,
+                pltpu.SemaphoreType.DMA((3,)),
+                pltpu.SemaphoreType.DMA((2,)),
             ],
             compiler_params=pltpu.CompilerParams(vmem_limit_bytes=30 * 1024 * 1024),
             name="verify_stream",
-        )(pltpu.with_memory_space_constraint(jnp.transpose(hidden, (1, 0, 2)), pltpu.HBM), norm_gain.reshape(1, depth), w_head.T,
-          temperature.reshape(1, seqs), tokens)
-        zs = streamed[0]
+        )(*[pltpu.with_memory_space_constraint(x, pltpu.HBM) for x in (
+            jnp.transpose(hidden, (1, 0, 2)), norm_gain.reshape(1, depth), w_head.T,
+            temperature.reshape(1, seqs), draft_tokens.T)])
 
         shared = pl.pallas_call(
             functools.partial(exchange_kernel, dims, n),
-            out_shape=(pltpu.VMEM((rows, vocab), F32), pltpu.VMEM((total, twide), F32),
-                       pltpu.VMEM((rows, LANES), F32), pltpu.VMEM((rows, LANES), F32),
+            out_shape=(pltpu.VMEM((rows, vocab), F32), pltpu.VMEM((rows, LANES), F32),
                        pltpu.VMEM((8, LANES), F32)),
             in_specs=[hbm] + [vmem] * 8,
-            out_specs=(vmem,) * 5,
+            out_specs=(vmem,) * 3,
             scratch_shapes=[
+                pltpu.VMEM((total, twide), F32),
+                pltpu.VMEM((rows, LANES), F32),
                 pltpu.VMEM((total, LANES), F32),
                 pltpu.VMEM((total, LANES), F32),
                 pltpu.VMEM((rows, LANES), F32),
                 pltpu.VMEM((rows, LANES), F32),
-                pltpu.VMEM((draft, LANES), jnp.int32),
                 pltpu.VMEM((4, LANES), F32),
                 pltpu.VMEM((n, 4, LANES), F32),
                 pltpu.VMEM((4, LANES), F32),
@@ -427,19 +446,21 @@
             compiler_params=pltpu.CompilerParams(
                 collective_id=0, has_side_effects=True, vmem_limit_bytes=6 * 1024 * 1024),
             name="verify_exchange",
-        )(pltpu.with_memory_space_constraint(draft_probs, pltpu.HBM), *held(streamed), tokens)
+        )(pltpu.with_memory_space_constraint(draft_probs, pltpu.HBM), *held(streamed))
 
         residual, accept, norm_sum, bonus = pl.pallas_call(
             functools.partial(write_kernel, dims),
             out_shape=(jax.ShapeDtypeStruct((seqs, draft, vocab), F32),
                        jax.ShapeDtypeStruct((draft, seqs), F32), jax.ShapeDtypeStruct((draft, seqs), F32),
                        jax.ShapeDtypeStruct((1, seqs), F32)),
-            in_specs=[vmem] * 6,
-            out_specs=(hbm, vmem, vmem, vmem),
-            scratch_shapes=[pltpu.VMEM((rows, vocab), F32), pltpu.SemaphoreType.DMA((seqs,))],
+            in_specs=[vmem] * 3,
+            out_specs=(hbm, hbm, hbm, hbm),
+            scratch_shapes=[pltpu.VMEM((draft, seqs), F32), pltpu.VMEM((draft, seqs), F32), pltpu.VMEM((1, seqs), F32),
+                            pltpu.VMEM((rows, vocab), F32), pltpu.SemaphoreType.DMA((seqs,)),
+                            pltpu.SemaphoreType.DMA((3,))],
             compiler_params=pltpu.CompilerParams(vmem_limit_bytes=10 * 1024 * 1024),
             name="verify_write",
-        )(*held((shared[0], zs) + tuple(shared[1:])))
+        )(*held(shared))
 
         return accept.T, norm_sum.T, residual, bonus.reshape(seqs)
 

time: 51.5 us -> 47.6 us (0.924)
  local copies, waits for them, and re-layouts: 2.05 us -> 0 us
  Pallas kernels: 48.6 us -> 46.8 us
    unnamed x6 -> x0, local copies, waits for them, and re-layouts: 2.05 us -> none
    pallas_call x1, Pallas kernels: 24.5 us -> 23.8 us  [local_step(): pl.pallas_call(functools.partial(stream_kernel, dims), out_shape=(pltpu.V...]
    pallas_call x1, Pallas kernels: 4.54 us -> 3.91 us  [local_step(): pl.pallas_call(functools.partial(write_kernel, dims), out_shape=(jax.Shap...]
where the time goes in v3:
time: 47.6 us; the launch traced here: 47.5 us
  Pallas kernels  46.8 us (98%)
  between operations  0.65 us (1%)
    pallas_call x1, Pallas kernels, local_step(): pl.pallas_call(functools.partial(stream_kernel, dims), out_shape=(pltpu.V...  23.8 us
    pallas_call x1, Pallas kernels, local_step(): pl.pallas_call(functools.partial(exchange_kernel, dims, n), out_shape=(pl...  19.1 us
    pallas_call x1, Pallas kernels, local_step(): pl.pallas_call(functools.partial(write_kernel, dims), out_shape=(jax.Shap...  3.91 us

profile of v3, /device:TPU:0, one launch (start us, length us, event | category | flops | bytes accessed | tf_op | source)
XLA Modules:
  0.0 47.5 jit_solution(1944049925459469939)
XLA Ops:
  0.6 23.8 %verify_stream.1 = (f32[256,7168]{1,0:T(8,128)S(1)}, bf16[320,4096]{1,0:T(8,128)(2,1)S(1)}, bf16[848,4096]{1,0:T(8,128)(2,1)S(1)}, f32[320,128]{1,0:T(8,128)S(1)...) custom-call(bf16[5,64,4096]{2,1,0:T(8,128)(2,1)} %bitcast.9, ...), custom_call_target="tpu_custom_call" | custom-call | tf_op jit(solution)/shard_map/verify_stream/pallas_call | solution.py:393
  24.4 19.1 %verify_exchange.1 = (f32[256,8016]{1,0:T(8,128)S(1)}, f32[256,128]{1,0:T(8,128)S(1)}, f32[8,128]{1,0:T(8,128)S(1)}) custom-call(f32[64,4,8016]{2,1,0:T(4,128)} %q_hbm.1, f32[256,7168]{1,0:T(8,128)S(1)} %get-tuple-element.19.zs_ref, bf16[320,4096]{1,0:T(8,128)(2,1)S(1)} %get-tuple-element.20.xb_ref, bf16[848,4096]{1,0:T(8,128)(2,1)S(1)} %get-tuple-element.21.wtail_ref, ...), custom_call_target="tpu_custom_call" | custom-call | tf_op jit(solution)/shard_map/verify_exchange/pallas_call | solution.py:423
  43.6 3.9 %verify_write.1 = (f32[64,4,8016]{2,1,0:T(4,128)}, f32[4,64]{1,0:T(4,128)}, f32[4,64]{1,0:T(4,128)}, f32[1,64]{1,0:T(1,128)}) custom-call(f32[256,8016]{1,0:T(8,128)S(1)} %get-tuple-element.27.exc_ref, f32[256,128]{1,0:T(8,128)S(1)} %get-tuple-element.28.icol_ref, f32[8,128]{1,0:T(8,128)S(1)} %get-tuple-element.29.stat_ref), custom_call_target="tpu_custom_call" | custom-call | tf_op jit(solution)/shard_map/verify_write/pallas_call | solution.py:451
